TPU v7x, 256 devices: a whole 4x4x8 slice. The times are simulated.
256 devices in a mesh: dp: 32 (over x, z), tensor: 8 (over y, core).
Axes of the slice: x: 4, y: 4, z: 8, core: 2. Of those that a mesh axis runs over, the one named last changes fastest.
Arguments:
- vis_rows: bfloat16 [8, 256, 2, 3200], P(None, 'dp', None, 'tensor'), may hold values from -6 to 6
- ln_gain: float32 [2, 3200], replicated, may hold values from 0.25 to 1.75
- ln_bias: float32 [2, 3200], replicated, may hold values from -3 to 3
- proj_weight: bfloat16 [3200, 2, 8192], P('dp', None, 'tensor'), may hold values from -0.078125 to 0.078125
- text_rows: bfloat16 [32, 384, 8192], P('dp', None, 'tensor'), may hold values from -8 to 8
- attn_gain: float32 [8192], replicated, may hold values from 0.25 to 1.75
- w_query: bfloat16 [8192, 4096], P('dp', 'tensor'), may hold values from -0.088388348 to 0.088388348
- key_value_weight: bfloat16 [8192, 2, 1024], P('dp', None, 'tensor'), may hold values from -0.088388348 to 0.088388348
- tile_counts: int32 [32], replicated, may hold values from 1 to 16, 256 in all
- image_offsets: int32 [32], P('dp'), may hold values from 0 to 256
Outputs:
- attn_context: bfloat16 [32, 384, 4096], P('dp', None, 'tensor')
Inputs may be any that keep to these rules, and one draw needn't show every extreme that they name: tile_counts counts all 256 tiles, and its largest entry is exactly 16.
All inputs are finite; a program needn't handle non-finite values.
Results may differ from a plain program's by a relative error of at most 0.0074.
Values may be sent and summed in bfloat16 or wider, within the bound.
No kernel may reach another device: no remote copies, remote signals or barrier semaphores. Data moves between devices by JAX's collectives and lax.ppermute only.
A program may use at most 128 MiB of HBM per device.

v0:
```python
import jax
import jax.numpy as jnp
from jax import lax
from jax.sharding import PartitionSpec as P

QUERY_HEADS = 32
KEY_VALUE_HEADS = 8
HEAD_WIDTH = 128
vision_epsilon = 1e-06
decoder_epsilon = 1e-05
rope_base = 500000.0


def from_everyone(array, axis):
    count = lax.axis_size(axis)
    return lax.all_to_all(
        jnp.broadcast_to(array[None], (count, *array.shape)), axis, 0, 0, tiled=True
    )


def laid_out(tiles, dim):
    shape = list(tiles.shape[1:])
    shape[dim] *= tiles.shape[0]
    return jnp.moveaxis(tiles, 0, dim).reshape(shape)


def gather_directly(array, axis, dim):
    tiles = from_everyone(array, axis)
    return laid_out(tiles, dim)


def sent_together(arrays, axis, dim, along):
    columns = [a.reshape(*a.shape[:along], -1) for a in arrays]
    both = jnp.concatenate(columns, axis=along)
    filled, at, finished = (lax.all_gather(both, axis, axis=dim, tiled=True), 0, [])
    for a, column in zip(arrays, columns):
        piece = filled[..., at : at + column.shape[along]]
        finished.append(piece.reshape(*piece.shape[:along], *a.shape[along:]))
        at += column.shape[along]
    return tuple(finished)


def apply_rotary(value_rows, position_indices):
    half_width = value_rows.shape[-1] // 2
    exponents = jnp.arange(half_width, dtype=jnp.float32) * (2.0 / value_rows.shape[-1])
    frequency = rope_base ** (-exponents)
    angles = position_indices.astype(jnp.float32)[:, None] * frequency[None, :]
    cosine = jnp.cos(angles)[:, None, :]
    sine = jnp.sin(angles)[:, None, :]
    first_half = value_rows[..., :half_width]
    second_half = value_rows[..., half_width:]
    return jnp.concatenate(
        [first_half * cosine - second_half * sine, second_half * cosine + first_half * sine],
        axis=-1,
    )


def layer_norm(value_rows, gain, bias_values):
    average = jnp.mean(value_rows, axis=(-2, -1), keepdims=True)
    centered = value_rows - average
    variance = jnp.mean(centered * centered, axis=(-2, -1), keepdims=True)
    return centered * lax.rsqrt(variance + vision_epsilon) * gain + bias_values


def attend(query_full, key_value_complete):
    seq_len = query_full.shape[0]
    query_group_count = QUERY_HEADS // KEY_VALUE_HEADS
    local_kv = key_value_complete.shape[2] // HEAD_WIDTH
    local_query = query_full.shape[1] // HEAD_WIDTH
    position_indices = jnp.arange(seq_len, dtype=jnp.int32)
    query_rows = apply_rotary(
        query_full.reshape(seq_len, local_query, HEAD_WIDTH), position_indices
    ).astype(jnp.bfloat16)
    query_rows = query_rows.reshape(seq_len, local_kv, query_group_count, HEAD_WIDTH)
    key_rows = apply_rotary(
        key_value_complete[:, 0].reshape(seq_len, local_kv, HEAD_WIDTH), position_indices
    ).astype(jnp.bfloat16)
    value_rows = (
        key_value_complete[:, 1].reshape(seq_len, local_kv, HEAD_WIDTH).astype(jnp.bfloat16)
    )
    scores = jnp.einsum(
        "pgjd,kgd->gjpk", query_rows, key_rows, preferred_element_type=jnp.float32
    ) * HEAD_WIDTH ** (-0.5)
    causal = position_indices[:, None] >= position_indices[None, :]
    scores = jnp.where(causal[None, None], scores, -1e30)
    row_max = jnp.max(scores, axis=-1, keepdims=True)
    exponentials = jnp.exp(scores - row_max)
    weights = (exponentials / jnp.sum(exponentials, axis=-1, keepdims=True)).astype(jnp.bfloat16)
    context = jnp.einsum("gjpk,kgd->pgjd", weights, value_rows, preferred_element_type=jnp.float32)
    return context.astype(jnp.bfloat16).reshape(seq_len, local_query * HEAD_WIDTH)


def per_device(
    vis_rows,
    ln_gain,
    ln_bias,
    proj_weight,
    text_rows,
    attn_gain,
    w_query,
    key_value_weight,
    tile_counts,
    image_offsets,
):
    data_count = lax.axis_size("dp")
    data_index = lax.axis_index("dp")
    tile_rows, tile_tok, merge_count, part_width = vis_rows.shape
    vision_width = ln_gain.shape[1]
    part_model = proj_weight.shape[2]
    token_count = tile_rows * tile_tok
    max_tiles = 2 * tile_rows
    slot_count = (max_tiles + data_count - 1) // data_count
    tile_ends = jnp.cumsum(tile_counts)
    tile_firsts = tile_ends - tile_counts
    sample_ids = jnp.arange(data_count, dtype=jnp.int32)
    tiles_here = jnp.arange(tile_rows, dtype=jnp.int32) * data_count + data_index
    owners = jnp.sum((tile_ends[None, :] <= tiles_here[:, None]).astype(jnp.int32), axis=1)
    owner_first = jnp.sum(
        jnp.where(sample_ids[None, :] == owners[:, None], tile_firsts[None, :], 0), axis=1
    )
    slots = (tiles_here - owner_first) // data_count
    is_mine = sample_ids == data_index
    my_first = jnp.sum(jnp.where(is_mine, tile_firsts, 0))
    my_count = jnp.sum(jnp.where(is_mine, tile_counts, 0))
    tile_order = jnp.arange(max_tiles, dtype=jnp.int32)
    sources = (my_first + tile_order) % data_count
    slot_index = tile_order // data_count
    image_span = max_tiles * tile_tok
    whole = gather_directly(vis_rows, "tensor", 3)
    merged = whole.reshape(token_count, merge_count, vision_width).astype(jnp.float32)
    normed_vis = layer_norm(merged, ln_gain, ln_bias).astype(jnp.bfloat16)
    columns = normed_vis
    image_cols = (
        jnp.einsum(
            "rmf,fmo->ro",
            columns,
            lax.all_gather(proj_weight, "dp", axis=0, tiled=True),
            preferred_element_type=jnp.float32,
        )
        .astype(jnp.bfloat16)
        .reshape(tile_rows, tile_tok, part_model)
    )
    empty_slots = jnp.zeros((data_count, slot_count) + image_cols.shape[1:], jnp.bfloat16)
    received = lax.all_to_all(
        empty_slots.at[owners, slots].set(image_cols), "dp", split_axis=0, concat_axis=0, tiled=True
    )
    arrived = received[sources, slot_index]
    arrived = arrived.reshape(image_span, part_model)
    start_row = image_offsets[0]
    sequence = text_rows[0]
    current = lax.dynamic_slice_in_dim(sequence, start_row, image_span, 0)
    is_image = jnp.repeat(tile_order < my_count, tile_tok)[:, None]
    combined = jnp.where(is_image, arrived, current)
    sequence = lax.dynamic_update_slice_in_dim(sequence, combined, start_row, 0)
    gathered = gather_directly(sequence, "tensor", 1)
    seq_float = gathered.astype(jnp.float32)
    mean_square = jnp.mean(seq_float * seq_float, axis=-1, keepdims=True)
    normalized_sequence = (seq_float * lax.rsqrt(mean_square + decoder_epsilon) * attn_gain).astype(
        jnp.bfloat16
    )
    seq_len = normalized_sequence.shape[0]
    weight_rows = sent_together((w_query, key_value_weight), "dp", 0, 1)
    columns = normalized_sequence
    query_part = jnp.dot(columns, weight_rows[0], preferred_element_type=jnp.float32)
    keyval_part = jnp.einsum(
        "sd,dck->sck", columns, weight_rows[1], preferred_element_type=jnp.float32
    )
    context = attend(query_part, keyval_part)
    return context.reshape(1, seq_len, context.shape[1])


def solution(mesh):
    in_specs = (
        P(None, "dp", None, "tensor"),
        P(),
        P(),
        P("dp", None, "tensor"),
        P("dp", None, "tensor"),
        P(),
        P("dp", "tensor"),
        P("dp", None, "tensor"),
        P(),
        P("dp"),
    )
    out_specs = P("dp", None, "tensor")
    return jax.shard_map(
        per_device, mesh=mesh, in_specs=in_specs, out_specs=out_specs, check_vma=False
    )
```

profile of v0, /device:TPU:1, one launch (start us, length us, event | category | flops | bytes accessed | tf_op | source)
XLA Modules:
  0.0 314.7 jit_solution(18428205670531530554)
XLA Ops:
  6.5 1.2 copy.86
  7.8 0.9 copy.81
  8.7 0.8 pad_maximum_fusion
  9.6 1.1 broadcast_in_dim.55
  10.7 6.7 %all-to-all-start = ((bf16[8,8,8,2,400]{4,2,1,3,0:T(8,128)(2,1)}), bf16[8,8,8,2,400]{4,2,1,3,0:T(8,128)(2,1)S(1)}, u32[]{:S(2)}, u32[]{:S(2)}) async-start(bf16[8,8,8,2,400]{4,2,1,3,0:T(8,128)(2,1)} %broadcast_in_dim.55), calls=%async_computation | async-start | bytes 2097152 | tf_op jit(solution)/shard_map/all_to_all | solution.py:16
  17.4 0.1 copy.51
  17.5 0.1 reduce.6
  17.6 0.2 convert_reduce_fusion
  17.8 0.7 fusion.48
  18.5 0.2 select_reduce_fusion
  18.7 13.6 %all-to-all-done = bf16[8,8,8,2,400]{4,2,1,3,0:T(8,128)(2,1)S(1)} async-done(((bf16[8,8,8,2,400]{4,2,1,3,0:T(8,128)(2,1)}), bf16[8,8,8,2,400]{4,2,1,3,0:T(8,128)(2,1)S(1)}, u32[]{:S(2)}, u32[]{:S(2)}) %all-to-all-start) | async-done | bytes 819232 | tf_op jit(solution)/shard_map/all_to_all | solution.py:16
  32.4 0.3 fusion.19
  32.6 0.1 div.47
  32.7 0.5 multiply_reduce_fusion
  33.2 0.1 rsqrt.20
  33.3 0.3 convert_bitcast_fusion
  33.6 1.6 copy.53
  35.2 2.3 reshape.465
  37.5 97.1 %all-gather.3.cloned.1.call-done = bf16[3200,2,1024]{2,1,0:T(2,128)(2,1)} async-done(((bf16[100,2,1024]{2,1,0:T(2,128)(2,1)}), bf16[3200,2,1024]{2,1,0:T(2,128)(2,1)}) %all-gather.3.cloned.1.call-update) | async-done | bytes 13107216 | tf_op jit(solution)/shard_map/all_gather | solution.py:137
  134.6 9.4 %fusion.16 = bf16[8,8,1024]{2,1,0:T(8,128)(2,1)S(1)} fusion(bf16[3200,2,1024]{2,1,0:T(2,128)(2,1)} %all-gather.3.cloned.1.call-done, f32[64,2,3200]{2,0,1:T(8,128)} %reshape.465, f32[2,3200]{1,0:T(2,128)S(1)} %copy-done.5, f32[2,3200]{1,0:T(2,128)S(1)} %copy-done.6, f32[64]{0:T(128)S(1)} %rsqrt.20, f32[64]{0:T(128)S(1)} %div.47), kind=kOutput, calls=%fused_computation.24 | convolution fusion | flops 840974336 | bytes 14928384 | tf_op jit(solution)/shard_map/rmf,fmo->ro/dot_general | solution.py:134
  144.0 0.9 broadcast.417
  144.9 2.1 scatter_fusion
  147.0 5.3 %all-to-all-start.1 = ((bf16[32,1,8,1024]{3,2,1,0:T(8,128)(2,1)}), bf16[32,1,8,1024]{3,2,1,0:T(8,128)(2,1)S(1)}, u32[]{:S(2)}, u32[]{:S(2)}) async-start(bf16[32,1,8,1024]{3,2,1,0:T(8,128)(2,1)} %bitcast.8), calls=%async_computation.1 | async-start | bytes 1048576 | tf_op jit(solution)/shard_map/all_to_all | solution.py:144
  153.0 0.7 iota_compare_fusion.2
  153.8 0.1 broadcast_in_dim.50
  153.9 0.6 fusion.46
  154.5 17.5 %all-to-all-done.1 = bf16[32,1,8,1024]{3,2,1,0:T(8,128)(2,1)S(1)} async-done(((bf16[32,1,8,1024]{3,2,1,0:T(8,128)(2,1)}), bf16[32,1,8,1024]{3,2,1,0:T(8,128)(2,1)S(1)}, u32[]{:S(2)}, u32[]{:S(2)}) %all-to-all-start.1) | async-done | bytes 524320 | tf_op jit(solution)/shard_map/all_to_all | solution.py:144
  172.0 0.6 gather_fusion
  172.6 0.1 fusion.28
  172.7 1.8 dynamic_update_slice.5
  174.5 3.4 %broadcast_in_dim.61 = bf16[8,384,1024]{2,1,0:T(8,128)(2,1)} broadcast(bf16[384,1024]{1,0:T(8,128)(2,1)S(1)} %dynamic_update_slice.5), dimensions={1,2} | broadcast | bytes 7077888 | tf_op jit(solution)/shard_map/broadcast_in_dim | solution.py:17
  177.9 8.6 %all-to-all-start.2 = ((bf16[8,384,1024]{2,1,0:T(8,128)(2,1)}), bf16[8,384,1024]{2,1,0:T(8,128)(2,1)}, u32[]{:S(2)}, u32[]{:S(2)}) async-start(bf16[8,384,1024]{2,1,0:T(8,128)(2,1)} %broadcast_in_dim.61), calls=%async_computation.2 | async-start | bytes 12582912 | tf_op jit(solution)/shard_map/all_to_all | solution.py:16
  186.6 0.4 multiply_cosine_fusion
  187.0 74.0 %all-gather.5.cloned.1.call-done = bf16[8192,768]{1,0:T(8,128)(2,1)} async-done(((bf16[256,768]{1,0:T(8,128)(2,1)}), bf16[8192,768]{1,0:T(8,128)(2,1)}) %all-gather.5.cloned.1.call-update) | async-done | bytes 12582928 | tf_op jit(solution)/shard_map/all_gather | solution.py:35
  261.0 7.1 %slice_bitcast_fusion = bf16[512,8192]{0,1:T(8,128)(2,1)} fusion(bf16[8192,768]{1,0:T(8,128)(2,1)} %all-gather.5.cloned.1.call-done), kind=kLoop, calls=%fused_computation.9 | loop fusion | bytes 16777216 | tf_op jit(solution)/shard_map/dot_general | solution.py:164
  268.1 11.9 %copy.58 = bf16[512,8192]{1,0:T(8,128)(2,1)} copy(bf16[512,8192]{0,1:T(8,128)(2,1)} %slice_bitcast_fusion) | data formatting | bytes 16777216 | tf_op jit(solution)/shard_map/dot_general | solution.py:164
  280.0 8.7 %copy.55 = bf16[8,384,1024]{1,2,0:T(8,128)(2,1)} copy(bf16[8,384,1024]{2,1,0:T(8,128)(2,1)} %all-to-all-done.2) | data formatting | bytes 12582912 | tf_op jit(solution)/shard_map/all_to_all | solution.py:16
  288.7 4.3 %fusion.2 = f32[384]{0:T(512)S(1)} fusion(bf16[8,384,1024]{1,2,0:T(8,128)(2,1)} %copy.55), kind=kLoop, calls=%fused_computation.6 | loop fusion | flops 9436800 | bytes 6292992 | tf_op jit(solution)/shard_map/reduce_sum | solution.py:157
  293.0 0.2 copy-done
  293.3 1.7 fusion.4
  295.0 4.8 %fusion.5 = f32[384,256]{0,1:S(1)} fusion(bf16[384,8192]{0,1:T(8,128)(2,1)S(1)} %bitcast.102, bf16[8192,768]{1,0:T(8,128)(2,1)} %all-gather.5.cloned.1.call-done), kind=kOutput, calls=%fused_computation.10 | convolution fusion | flops 1610612736 | bytes 10878976
  299.8 0.4 fusion.42
  300.3 4.5 %fusion.56 = f32[384,4,128]{0,2,1:T(8,128)S(1)} fusion(bf16[384,8192,1]{0,1,2:T(8,128)(2,1)S(1)} %bitcast.103, bf16[4,128,8192]{2,1,0:T(8,128)(2,1)S(1)} %bitcast.101), kind=kOutput, calls=%fused_computation.102 | convolution fusion | flops 3221225472 | bytes 15466496 | tf_op jit(solution)/shard_map/dot_general | solution.py:164
  304.8 0.1 subtract_convert_fusion
  304.9 0.6 fusion.8
  305.5 0.5 fusion.7
  306.0 0.9 convolution_convert_fusion
  306.9 0.9 copy.63
  (35 shorter events, 0.4 us)
Async XLA Ops:
  6.5 3.0 copy-start.2
  6.5 2.2 copy-start.1
  6.5 128.0 %all-gather.3.cloned.1.call-start = ((), (), s32[]{:S(2)}) async-start(), calls=%async_computation.3 | async-start | bytes 13516800 | tf_op jit(solution)/shard_map/all_gather | solution.py:137
  7.8 253.2 %all-gather.5.cloned.1.call-start = ((), (), s32[]{:S(2)}) async-start(), calls=%async_computation.4 | async-start | bytes 12976128 | tf_op jit(solution)/shard_map/all_gather | solution.py:35
  8.7 8.6 %copy-start.4 = (s32[32]{0:T(128)S(1)}, s32[32]{0:T(128)}, u32[]{:S(2)}) copy-start(s32[32]{0:T(128)} %param.18) | copy-start | bytes 388
  10.7 21.7 %all-to-all-start = ((bf16[8,8,8,2,400]{4,2,1,3,0:T(8,128)(2,1)}), bf16[8,8,8,2,400]{4,2,1,3,0:T(8,128)(2,1)S(1)}, u32[]{:S(2)}, u32[]{:S(2)}) async-start(bf16[8,8,8,2,400]{4,2,1,3,0:T(8,128)(2,1)} %broadcast_in_dim.55), calls=%async_computation | async-start | bytes 2097152 | tf_op jit(solution)/shard_map/all_to_all | solution.py:16
  35.2 99.4 %copy-start.5 = (f32[2,3200]{1,0:T(2,128)S(1)}, f32[2,3200]{1,0:T(2,128)}, u32[]{:S(2)}) copy-start(f32[2,3200]{1,0:T(2,128)} %param.12) | copy-start | bytes 76804
  35.2 99.4 %copy-start.6 = (f32[2,3200]{1,0:T(2,128)S(1)}, f32[2,3200]{1,0:T(2,128)}, u32[]{:S(2)}) copy-start(f32[2,3200]{1,0:T(2,128)} %param.11) | copy-start | bytes 76804
  147.0 25.0 %all-to-all-start.1 = ((bf16[32,1,8,1024]{3,2,1,0:T(8,128)(2,1)}), bf16[32,1,8,1024]{3,2,1,0:T(8,128)(2,1)S(1)}, u32[]{:S(2)}, u32[]{:S(2)}) async-start(bf16[32,1,8,1024]{3,2,1,0:T(8,128)(2,1)} %bitcast.8), calls=%async_computation.1 | async-start | bytes 1048576 | tf_op jit(solution)/shard_map/all_to_all | solution.py:144
  177.9 8.6 %copy-start.3 = (f32[8192]{0:T(1024)S(1)}, f32[8192]{0:T(1024)}, u32[]{:S(2)}) copy-start(f32[8192]{0:T(1024)} %param.15) | copy-start | bytes 98308
  177.9 102.1 %all-to-all-start.2 = ((bf16[8,384,1024]{2,1,0:T(8,128)(2,1)}), bf16[8,384,1024]{2,1,0:T(8,128)(2,1)}, u32[]{:S(2)}, u32[]{:S(2)}) async-start(bf16[8,384,1024]{2,1,0:T(8,128)(2,1)} %broadcast_in_dim.61), calls=%async_computation.2 | async-start | bytes 12582912 | tf_op jit(solution)/shard_map/all_to_all | solution.py:16
  288.7 4.6 %copy-start = (bf16[8,384,1024]{1,2,0:T(8,128)(2,1)S(1)}, bf16[8,384,1024]{1,2,0:T(8,128)(2,1)}, u32[]{:S(2)}) copy-start(bf16[8,384,1024]{1,2,0:T(8,128)(2,1)} %copy.55) | copy-start | bytes 18874372
  293.3 7.0 %slice-start = ((s8[8388608]{0:T(1024)(128)(4,1)}), s8[4194304]{0:T(1024)(128)(4,1)S(1)}, s32[]{:S(2)}) async-start(s8[8388608]{0:T(1024)(128)(4,1)} %bitcast.99), calls=%async_computation.5 | async-start | bytes 8388608
  295.0 5.2 %slice-start.1 = ((s8[8388608]{0:T(1024)(128)(4,1)}), s8[4194304]{0:T(1024)(128)(4,1)S(1)}, s32[]{:S(2)}) async-start(s8[8388608]{0:T(1024)(128)(4,1)} %bitcast.99), calls=%async_computation.6 | async-start | bytes 8388608
Sparse Core Ops, SparseCore 0:
  9.9 124.6 all-gather.2
  137.2 123.7 all-gather.4
where the time goes:
time: 316 us; the launch traced here: 315 us
  waiting for transfers between devices  202 us (64%)
  local copies, waits for them, and re-layouts  45.2 us (14%)
  starting transfers between devices  20.6 us (7%)
  matrix products  20.2 us (6%)
  between operations  14.3 us (5%)
  other arithmetic  12.2 us (4%)
    all_gather x1, waiting for transfers between devices, per_device(): lax.all_gather(proj_weight, 'dp', axis=0, tiled=True)  97.1 us
    all_gather x1, waiting for transfers between devices, sent_together(): lax.all_gather(both, axis, axis=dim, tiled=True)  74 us
    dot_general x2, local copies, waits for them, and re-layouts, per_device(): jnp.dot(columns, weight_rows[0], preferred_element_type=jnp.float32)  19 us
    all_to_all x1, waiting for transfers between devices, per_device(): lax.all_to_all(empty_slots.at[owners, slots].set(image_cols), 'dp', split...  17.5 us
    all_to_all x2, starting transfers between devices, from_everyone(): lax.all_to_all(jnp.broadcast_to(array[None], (count, *array.shape)), axis...  15.2 us
    all_to_all x2, waiting for transfers between devices, from_everyone(): lax.all_to_all(jnp.broadcast_to(array[None], (count, *array.shape)), axis...  13.6 us
    dot_general x1, matrix products, per_device(): jnp.einsum('rmf,fmo->ro', columns, lax.all_gather(proj_weight, 'dp', axis...  9.42 us
    all_to_all x1, local copies, waits for them, and re-layouts, from_everyone(): lax.all_to_all(jnp.broadcast_to(array[None], (count, *array.shape)), axis...  8.65 us
  transfers between devices with their start and end apart: 5, of which 4 were waited for; matrix products, arithmetic and copies ran while one was open for 15% of the time, Pallas kernels for 0%

commit v1 on v0

--- a/solution.py
+++ b/solution.py
@@ -9,6 +9,12 @@
 vision_epsilon = 1e-06
 decoder_epsilon = 1e-05
 rope_base = 500000.0
+
+
+def gather_from_all(x, axis, dim):
+    peers = lax.axis_size(axis)
+    repeats = [peers if d == dim else 1 for d in range(x.ndim)]
+    return lax.all_to_all(jnp.tile(x, repeats), axis, split_axis=dim, concat_axis=dim, tiled=True)
 
 
 def from_everyone(array, axis):
@@ -134,7 +140,7 @@
         jnp.einsum(
             "rmf,fmo->ro",
             columns,
-            lax.all_gather(proj_weight, "dp", axis=0, tiled=True),
+            gather_from_all(proj_weight, "dp", 0),
             preferred_element_type=jnp.float32,
         )
         .astype(jnp.bfloat16)

time: 316 us -> 576 us (1.82)
  waiting for transfers between devices: 202 us -> 420 us
  blocking collectives: 0 us -> 20.7 us
  local copies, waits for them, and re-layouts: 45.2 us -> 57.1 us
  starting transfers between devices: 20.6 us -> 30 us
    all_to_all x0 -> x1, waiting for transfers between devices: none -> 358 us  [gather_from_all(): lax.all_to_all(jnp.tile(x, repeats), axis, split_axis=dim, concat_axis=di...]
    all_gather x1 -> x0, waiting for transfers between devices: 97.1 us -> none  [per_device(): lax.all_gather(proj_weight, 'dp', axis=0, tiled=True)]
    all_gather x1, waiting for transfers between devices: 74 us -> 0.02 us  [sent_together(): lax.all_gather(both, axis, axis=dim, tiled=True)]
    all_to_all x2 -> x1, waiting for transfers between devices: 13.6 us -> 51.7 us  [from_everyone(): lax.all_to_all(jnp.broadcast_to(array[None], (count, *array.shape)), axis...]
    all_to_all x0 -> x1, blocking collectives: none -> 20.7 us  [from_everyone(): lax.all_to_all(jnp.broadcast_to(array[None], (count, *array.shape)), axis...]
    another operation x1 -> x2, local copies, waits for them, and re-layouts: 0.09 us -> 13 us  [the longest x1 12.9 us: gather_from_all(): jnp.tile(x, repeats)]
    all_to_all x0 -> x1, starting transfers between devices: none -> 11.3 us  [gather_from_all(): lax.all_to_all(jnp.tile(x, repeats), axis, split_axis=dim, concat_axis=di...]
    all_to_all x1, waiting for transfers between devices: 17.5 us -> 10.9 us  [per_device(): lax.all_to_all(empty_slots.at[owners, slots].set(image_cols), 'dp', split...]
  transfers between devices with their start and end apart: 5 -> 4, of which waited for: 4 -> 3; matrix products, arithmetic and copies ran while one was open for 15% -> 8% of each run, Pallas kernels for 0% -> 0%
where the time goes in v1:
time: 576 us; the launch traced here: 575 us
  waiting for transfers between devices  420 us (73%)
  local copies, waits for them, and re-layouts  57.1 us (10%)
  starting transfers between devices  30 us (5%)
  blocking collectives  20.7 us (4%)
  matrix products  20.2 us (4%)
  between operations  14.3 us (2%)
  other arithmetic  12.2 us (2%)
    all_to_all x1, waiting for transfers between devices, gather_from_all(): lax.all_to_all(jnp.tile(x, repeats), axis, split_axis=dim, concat_axis=di...  358 us
    all_to_all x1, waiting for transfers between devices, from_everyone(): lax.all_to_all(jnp.broadcast_to(array[None], (count, *array.shape)), axis...  51.7 us
    all_to_all x1, blocking collectives, from_everyone(): lax.all_to_all(jnp.broadcast_to(array[None], (count, *array.shape)), axis...  20.7 us
    dot_general x2, local copies, waits for them, and re-layouts, per_device(): jnp.dot(columns, weight_rows[0], preferred_element_type=jnp.float32)  19 us
    another operation x1, local copies, waits for them, and re-layouts, gather_from_all(): jnp.tile(x, repeats)  12.9 us
  transfers between devices with their start and end apart: 4, of which 3 were waited for; matrix products, arithmetic and copies ran while one was open for 8% of the time, Pallas kernels for 0%

profile of v1, /device:TPU:1, one launch (start us, length us, event | category | flops | bytes accessed | tf_op | source)
XLA Modules:
  0.0 574.8 jit_solution(11031413764469781988)
XLA Ops:
  6.5 1.2 copy.94
  7.7 0.9 copy.56
  8.6 0.1 broadcast_in_dim.55
  8.7 20.7 %all_to_all.20 = bf16[8,8,8,2,400]{4,2,1,3,0:T(8,128)(2,1)S(1)} all-to-all(bf16[8,8,8,2,400]{4,2,1,3,0:T(8,128)(2,1)S(1)} %broadcast_in_dim.55), channel_id=1, replica_groups=mesh['dp'=32,'tensor'=8] {'tensor'}, dimensions={0} | all-to-all | bytes 1638400 | tf_op jit(solution)/shard_map/all_to_all | solution.py:22
  29.4 12.9 %tile.4.clone = bf16[32,100,2,1024]{3,2,1,0:T(2,128)(2,1)} broadcast(bf16[100,2,1024]{2,1,0:T(2,128)(2,1)S(1)} %copy-done.1), dimensions={1,2,3} | broadcast | bytes 13516800 | tf_op jit(solution)/shard_map/tile | solution.py:17
  42.4 11.3 %all-to-all-start.1 = ((bf16[3200,2,1024]{2,1,0:T(2,128)(2,1)}), bf16[3200,2,1024]{2,1,0:T(2,128)(2,1)}, u32[]{:S(2)}, u32[]{:S(2)}) async-start(bf16[3200,2,1024]{2,1,0:T(2,128)(2,1)} %bitcast.99), calls=%async_computation.1 | async-start | bytes 26214400 | tf_op jit(solution)/shard_map/all_to_all | solution.py:17
  53.8 0.8 pad_maximum_fusion
  54.6 0.1 copy.55
  54.7 0.1 reduce.6
  54.9 0.2 convert_reduce_fusion
  55.0 0.7 fusion.48
  55.7 0.2 select_reduce_fusion
  56.0 0.3 fusion.19
  56.2 0.1 div.47
  56.3 0.5 multiply_reduce_fusion
  56.9 0.3 convert_bitcast_fusion
  57.1 1.6 copy.57
  58.8 2.2 reshape.469
  61.0 357.8 %all-to-all-done.1 = bf16[3200,2,1024]{2,1,0:T(2,128)(2,1)} async-done(((bf16[3200,2,1024]{2,1,0:T(2,128)(2,1)}), bf16[3200,2,1024]{2,1,0:T(2,128)(2,1)}, u32[]{:S(2)}, u32[]{:S(2)}) %all-to-all-start.1) | async-done | bytes 13107232 | tf_op jit(solution)/shard_map/all_to_all | solution.py:17
  418.9 9.4 %fusion.16 = bf16[8,8,1024]{2,1,0:T(8,128)(2,1)S(1)} fusion(bf16[3200,2,1024]{2,1,0:T(2,128)(2,1)} %all-to-all-done.1, f32[64,2,3200]{2,0,1:T(8,128)} %reshape.469, f32[2,3200]{1,0:T(2,128)S(1)} %copy-done.6, f32[2,3200]{1,0:T(2,128)S(1)} %copy-done.7, f32[64]{0:T(128)S(1)} %rsqrt.20, f32[64]{0:T(128)S(1)} %div.47), kind=kOutput, calls=%fused_computation.24 | convolution fusion | flops 840974336 | bytes 14928384 | tf_op jit(solution)/shard_map/rmf,fmo->ro/dot_general | solution.py:140
  428.3 0.9 broadcast.420
  429.2 2.1 scatter_fusion
  431.3 8.8 %all-to-all-start.2 = ((bf16[32,1,8,1024]{3,2,1,0:T(8,128)(2,1)}), bf16[32,1,8,1024]{3,2,1,0:T(8,128)(2,1)S(1)}, u32[]{:S(2)}, u32[]{:S(2)}) async-start(bf16[32,1,8,1024]{3,2,1,0:T(8,128)(2,1)} %bitcast.9), calls=%async_computation.2 | async-start | bytes 1048576 | tf_op jit(solution)/shard_map/all_to_all | solution.py:150
  440.7 0.7 iota_compare_fusion.2
  441.4 0.1 broadcast_in_dim.50
  441.5 0.6 fusion.46
  442.2 10.9 %all-to-all-done.2 = bf16[32,1,8,1024]{3,2,1,0:T(8,128)(2,1)S(1)} async-done(((bf16[32,1,8,1024]{3,2,1,0:T(8,128)(2,1)}), bf16[32,1,8,1024]{3,2,1,0:T(8,128)(2,1)S(1)}, u32[]{:S(2)}, u32[]{:S(2)}) %all-to-all-start.2) | async-done | bytes 524320 | tf_op jit(solution)/shard_map/all_to_all | solution.py:150
  453.0 0.6 gather_fusion
  453.6 0.1 fusion.28
  453.8 1.8 dynamic_update_slice.5
  455.5 3.4 broadcast_in_dim.61
  458.9 9.9 %all-to-all-start.3 = ((bf16[8,384,1024]{2,1,0:T(8,128)(2,1)}), bf16[8,384,1024]{2,1,0:T(8,128)(2,1)}, u32[]{:S(2)}, u32[]{:S(2)}) async-start(bf16[8,384,1024]{2,1,0:T(8,128)(2,1)} %broadcast_in_dim.61), calls=%async_computation.3 | async-start | bytes 12582912 | tf_op jit(solution)/shard_map/all_to_all | solution.py:22
  468.9 0.4 multiply_cosine_fusion
  469.4 7.1 %slice_bitcast_fusion = bf16[512,8192]{0,1:T(8,128)(2,1)} fusion(bf16[8192,768]{1,0:T(8,128)(2,1)} %all-gather.2.cloned.1.call-done), kind=kLoop, calls=%fused_computation.9 | loop fusion | bytes 16777216 | tf_op jit(solution)/shard_map/dot_general | solution.py:170
  476.5 11.9 %copy.64 = bf16[512,8192]{1,0:T(8,128)(2,1)} copy(bf16[512,8192]{0,1:T(8,128)(2,1)} %slice_bitcast_fusion) | data formatting | bytes 16777216 | tf_op jit(solution)/shard_map/dot_general | solution.py:170
  488.4 51.7 %all-to-all-done.3 = bf16[8,384,1024]{2,1,0:T(8,128)(2,1)} async-done(((bf16[8,384,1024]{2,1,0:T(8,128)(2,1)}), bf16[8,384,1024]{2,1,0:T(8,128)(2,1)}, u32[]{:S(2)}, u32[]{:S(2)}) %all-to-all-start.3) | async-done | bytes 6291488 | tf_op jit(solution)/shard_map/all_to_all | solution.py:22
  540.1 8.7 %copy.61 = bf16[8,384,1024]{1,2,0:T(8,128)(2,1)} copy(bf16[8,384,1024]{2,1,0:T(8,128)(2,1)} %all-to-all-done.3) | data formatting | bytes 12582912 | tf_op jit(solution)/shard_map/all_to_all | solution.py:22
  548.7 4.3 fusion.2
  553.1 0.2 copy-done
  553.3 1.7 fusion.4
  555.1 4.8 fusion.5
  559.9 0.4 fusion.42
  560.4 4.5 fusion.56
  564.8 0.1 subtract_convert_fusion
  565.0 0.6 fusion.8
  565.6 0.5 fusion.7
  566.1 0.9 convolution_convert_fusion
  567.0 0.9 copy.69
  (36 shorter events, 0.5 us)
Async XLA Ops:
  6.5 22.9 %copy-start.1 = (bf16[100,2,1024]{2,1,0:T(2,128)(2,1)S(1)}, bf16[100,2,1024]{2,1,0:T(2,128)(2,1)}, u32[]{:S(2)}) copy-start(bf16[100,2,1024]{2,1,0:T(2,128)(2,1)} %param.13) | copy-start | bytes 1228804
  42.4 11.4 %copy-start.3 = (bf16[256,2,128]{2,1,0:T(2,128)(2,1)S(1)}, bf16[256,2,128]{2,1,0:T(2,128)(2,1)}, u32[]{:S(2)}) copy-start(bf16[256,2,128]{2,1,0:T(2,128)(2,1)} %param.17) | copy-start | bytes 393220
  42.4 11.4 %copy-start.2 = (bf16[256,512]{1,0:T(8,128)(2,1)S(1)}, bf16[256,512]{1,0:T(8,128)(2,1)}, u32[]{:S(2)}) copy-start(bf16[256,512]{1,0:T(8,128)(2,1)} %param.16) | copy-start | bytes 786436
  42.4 12.2 %copy-start.5 = (s32[32]{0:T(128)S(1)}, s32[32]{0:T(128)}, u32[]{:S(2)}) copy-start(s32[32]{0:T(128)} %param.18) | copy-start | bytes 388
  42.4 376.5 %all-to-all-start.1 = ((bf16[3200,2,1024]{2,1,0:T(2,128)(2,1)}), bf16[3200,2,1024]{2,1,0:T(2,128)(2,1)}, u32[]{:S(2)}, u32[]{:S(2)}) async-start(bf16[3200,2,1024]{2,1,0:T(2,128)(2,1)} %bitcast.99), calls=%async_computation.1 | async-start | bytes 26214400 | tf_op jit(solution)/shard_map/all_to_all | solution.py:17
  53.7 415.7 %all-gather.2.cloned.1.call-start = ((), (), s32[]{:S(2)}) async-start(), calls=%async_computation.4 | async-start | bytes 12976128 | tf_op jit(solution)/shard_map/all_gather | solution.py:41
  58.8 360.1 %copy-start.6 = (f32[2,3200]{1,0:T(2,128)S(1)}, f32[2,3200]{1,0:T(2,128)}, u32[]{:S(2)}) copy-start(f32[2,3200]{1,0:T(2,128)} %param.12) | copy-start | bytes 76804
  58.8 360.0 %copy-start.7 = (f32[2,3200]{1,0:T(2,128)S(1)}, f32[2,3200]{1,0:T(2,128)}, u32[]{:S(2)}) copy-start(f32[2,3200]{1,0:T(2,128)} %param.11) | copy-start | bytes 76804
  431.3 21.8 %all-to-all-start.2 = ((bf16[32,1,8,1024]{3,2,1,0:T(8,128)(2,1)}), bf16[32,1,8,1024]{3,2,1,0:T(8,128)(2,1)S(1)}, u32[]{:S(2)}, u32[]{:S(2)}) async-start(bf16[32,1,8,1024]{3,2,1,0:T(8,128)(2,1)} %bitcast.9), calls=%async_computation.2 | async-start | bytes 1048576 | tf_op jit(solution)/shard_map/all_to_all | solution.py:150
  458.9 9.9 %copy-start.4 = (f32[8192]{0:T(1024)S(1)}, f32[8192]{0:T(1024)}, u32[]{:S(2)}) copy-start(f32[8192]{0:T(1024)} %param.15) | copy-start | bytes 98308
  458.9 81.2 %all-to-all-start.3 = ((bf16[8,384,1024]{2,1,0:T(8,128)(2,1)}), bf16[8,384,1024]{2,1,0:T(8,128)(2,1)}, u32[]{:S(2)}, u32[]{:S(2)}) async-start(bf16[8,384,1024]{2,1,0:T(8,128)(2,1)} %broadcast_in_dim.61), calls=%async_computation.3 | async-start | bytes 12582912 | tf_op jit(solution)/shard_map/all_to_all | solution.py:22
  548.7 4.6 copy-start
  553.3 7.0 %slice-start = ((s8[8388608]{0:T(1024)(128)(4,1)}), s8[4194304]{0:T(1024)(128)(4,1)S(1)}, s32[]{:S(2)}) async-start(s8[8388608]{0:T(1024)(128)(4,1)} %bitcast.100), calls=%async_computation.5 | async-start | bytes 8388608
  555.1 5.2 slice-start.1
Sparse Core Ops, SparseCore 0:
  57.1 300.5 all-gather.1
